TPU v7x, 32 devices: a whole 2x2x4 slice. The times are simulated.
32 devices in a mesh: dp: 8 (over z, y), seq: 4 (over x, core).
Axes of the slice: x: 2, y: 2, z: 4, core: 2. Of those that a mesh axis runs over, the one named last changes fastest.
Arguments:
- tokens: bfloat16 [16, 1024, 1536], P('dp', 'seq'), may hold values from -6 to 6
- in_proj: bfloat16 [1536, 6448], P(('dp', 'seq')), may hold values from -0.15625 to 0.15625
- conv_weight: bfloat16 [4, 3328], P(None, ('dp', 'seq')), may hold values from -3 to 3
- conv_bias: bfloat16 [3328], P(('dp', 'seq')), may hold values from -0.5 to 0.5
- decay_log: float32 [48], replicated, may hold values from -6 to 0.5
- step_bias: float32 [48], replicated, may hold values from -4.5 to -2
- skip_gain: float32 [48], replicated, may hold values from 0.5 to 1.5
- norm_gain: bfloat16 [1536], P(('dp', 'seq')), may hold values from 0.099609375 to 1.8984375
- gated_gain: bfloat16 [3072], P(('dp', 'seq')), may hold values from 0.099609375 to 1.8984375
- out_proj: bfloat16 [3072, 1536], P(('dp', 'seq')), may hold values from -0.109375 to 0.109375
- cotangent: bfloat16 [16, 1024, 1536], P('dp', 'seq'), may hold values from -6 to 6
Outputs:
- block_out: bfloat16 [16, 1024, 1536], P('dp', 'seq')
- tokens_grad: bfloat16 [16, 1024, 1536], P('dp', 'seq')
- in_proj_grad: float32 [1536, 6448], P(('dp', 'seq'))
- conv_weight_grad: float32 [4, 3328], P(None, ('dp', 'seq'))
- conv_bias_grad: float32 [3328], P(('dp', 'seq'))
- decay_log_grad: float32 [48], replicated
- step_bias_grad: float32 [48], replicated
- skip_gain_grad: float32 [48], replicated
- norm_gain_grad: float32 [1536], P(('dp', 'seq'))
- gated_gain_grad: float32 [3072], P(('dp', 'seq'))
- out_proj_grad: float32 [3072, 1536], P(('dp', 'seq'))
All inputs are finite; a program needn't handle non-finite values.
Results may differ from a plain program's by a relative error of at most 0.0062.
Values may be sent and summed in bfloat16 or wider, within the bound.
A program may use at most 256 MiB of HBM per device.

v0:
```python
import jax
import jax.numpy as jnp
from jax import lax
from jax.sharding import PartitionSpec as P

HEADS = 48
P_SIZE = 64
N = 128
KW = 4
GROUP = 256
DI = 3072
CD = 3328
EPSILON = 1e-05
precise = lax.Precision.HIGHEST


def shifted(shard, axis, by):
    peers = lax.axis_size(axis)
    pairs = [(i, i + by) for i in range(peers) if 0 <= i + by < peers]
    return lax.ppermute(shard, axis, pairs)


def entering_2(shard, axis, combine, identity, reverse):
    peers, mine = (lax.axis_size(axis), lax.axis_index(axis))
    everything = jax.tree.map(lambda part: lax.all_gather(part, axis), shard)
    start = jax.tree.map(
        lambda part, zero: jnp.broadcast_to(jnp.asarray(zero, part.dtype), part.shape),
        shard,
        identity,
    )

    def lap(k, before):
        at = peers - 1 - k if reverse else k
        reached = at > mine if reverse else at < mine
        new = combine(before, jax.tree.map(lambda part: part[at], everything))
        return jax.tree.map(lambda a, b: jnp.where(reached, a, b), new, before)

    return lax.fori_loop(0, peers, lap, start)


def group_step(memory, pieces):
    values, inputs_b, inputs_c, step_sizes, decays = pieces
    running = jnp.cumsum(decays, axis=0)
    blocks = decays.shape[0]
    causal = (jnp.arange(blocks)[:, None] >= jnp.arange(blocks)[None, :])[:, :, None]
    spread = running[:, None, :] - running[None, :, :]
    within = jnp.where(causal, jnp.exp(jnp.where(causal, spread, 0.0)), 0.0)
    scores = jnp.dot(inputs_c, inputs_b.T, precision=precise)
    weights = scores[:, :, None] * within * step_sizes[None, :, :]
    output = jnp.einsum("ijh,jhp->ihp", weights, values, precision=precise)
    output = output + jnp.exp(running)[:, :, None] * jnp.einsum(
        "in,hpn->ihp", inputs_c, memory, precision=precise
    )
    closing = running[-1]
    carried = jnp.exp(closing[None, :] - running) * step_sizes
    memory = memory * jnp.exp(closing)[:, None, None] + jnp.einsum(
        "jh,jhp,jn->hpn", carried, values, inputs_b, precision=precise
    )
    return (memory, output)


def local_mixer(projected, halo_rows, conv_weight, conv_bias, decay_log, step_bias, skip_gain):
    length = projected.shape[0]
    gate_half = projected[:, :DI]
    stream = projected[:, DI : DI + CD]
    raw_step = projected[:, DI + CD :]
    padded = jnp.concatenate([halo_rows, stream], axis=0)
    mixed_conv = conv_bias + jnp.zeros_like(stream)
    for offset in range(KW):
        mixed_conv = mixed_conv + conv_weight[offset] * padded[offset : offset + length]
    active = jax.nn.silu(mixed_conv)
    values = active[:, :DI].reshape(length, HEADS, P_SIZE)
    inputs_b = active[:, DI : DI + N]
    inputs_c = active[:, DI + N :]
    step_sizes = jax.nn.softplus(raw_step + step_bias)
    decays = -jnp.exp(decay_log) * step_sizes
    running = jnp.cumsum(decays, axis=0)
    blocks = length // GROUP
    pieces = tuple(
        (
            item.reshape((blocks, GROUP) + item.shape[1:])
            for item in (values, inputs_b, inputs_c, step_sizes, decays)
        )
    )
    memory = jnp.zeros((HEADS, P_SIZE, N), jnp.float32)
    closing, outputs = lax.scan(group_step, memory, pieces)
    partial_out = outputs.reshape(values.shape) + skip_gain[:, None] * values
    return (gate_half, partial_out, closing, running[-1], running, inputs_c)


def prenorm(inputs, norm_gain):
    inv_scale = lax.rsqrt(jnp.mean(inputs * inputs, axis=-1, keepdims=True) + EPSILON)
    return inputs * inv_scale * norm_gain


def gated_norm(ssd_out, gate_half, gated_gain):
    gated = ssd_out.reshape(ssd_out.shape[0], DI) * jax.nn.silu(gate_half)
    gated_scale = lax.rsqrt(jnp.mean(gated * gated, axis=-1, keepdims=True) + EPSILON)
    return gated * gated_scale * gated_gain


def combine(earlier, later):
    return (earlier[0] * later[1][:, None, None] + later[0], earlier[1] * later[1])


def collect(in_proj, conv_weight, conv_bias, norm_gain, gated_gain, out_proj):
    return (
        lax.all_gather(in_proj, ("dp", "seq"), axis=0, tiled=True),
        lax.all_gather(conv_weight, ("dp", "seq"), axis=1, tiled=True),
        lax.all_gather(conv_bias, ("dp", "seq"), axis=0, tiled=True),
        lax.all_gather(norm_gain, ("dp", "seq"), axis=0, tiled=True),
        lax.all_gather(gated_gain, ("dp", "seq"), axis=0, tiled=True),
        lax.all_gather(out_proj, ("dp", "seq"), axis=0, tiled=True),
    )


def share_out(grad_in, grad_conv, grad_bias, grad_norm, grad_gated, grad_out):
    return (
        lax.psum_scatter(grad_in, ("dp", "seq"), scatter_dimension=0, tiled=True),
        lax.psum_scatter(grad_conv, ("dp", "seq"), scatter_dimension=1, tiled=True),
        lax.psum_scatter(grad_bias, ("dp", "seq"), scatter_dimension=0, tiled=True),
        lax.psum_scatter(grad_norm, ("dp", "seq"), scatter_dimension=0, tiled=True),
        lax.psum_scatter(grad_gated, ("dp", "seq"), scatter_dimension=0, tiled=True),
        lax.psum_scatter(grad_out, ("dp", "seq"), scatter_dimension=0, tiled=True),
    )


def body(
    tokens,
    in_proj,
    conv_weight,
    conv_bias,
    decay_log,
    step_bias,
    skip_gain,
    norm_gain,
    gated_gain,
    out_proj,
    cotangent,
):
    micro_count = tokens.shape[0]
    length = tokens.shape[1]
    edge = length - (KW - 1)
    totals = None
    shares = None
    head_totals = (
        jnp.zeros((HEADS,), jnp.float32),
        jnp.zeros((HEADS,), jnp.float32),
        jnp.zeros((HEADS,), jnp.float32),
    )
    block_rows = []
    grad_rows = []
    for micro_index in range(micro_count):
        gathered = collect(in_proj, conv_weight, conv_bias, norm_gain, gated_gain, out_proj)
        w_in, w_conv, b_conv, g_norm, g_gated, w_out = gathered
        inputs = tokens[micro_index].astype(jnp.float32)
        normed_full, norm_back = jax.vjp(prenorm, inputs, g_norm.astype(jnp.float32))
        normed = normed_full.astype(jnp.bfloat16)
        projected = jnp.dot(normed, w_in, preferred_element_type=jnp.float32)
        tail_rows = projected[edge:, DI : DI + CD]
        halo_rows = shifted(tail_rows, "seq", 1)
        mixer_out, mixer_back = jax.vjp(
            local_mixer,
            projected,
            halo_rows,
            w_conv.astype(jnp.float32),
            b_conv.astype(jnp.float32),
            decay_log,
            step_bias,
            skip_gain,
        )
        gate_half, partial_out, closing, total_log, running, inputs_c = mixer_out
        decay_total = jnp.exp(total_log)
        entering, _ = entering_2(
            (closing, decay_total),
            "seq",
            combine,
            (jnp.zeros_like(closing), jnp.ones_like(decay_total)),
            False,
        )
        growth = jnp.exp(running)
        inherited = jnp.einsum("tn,hpn->thp", inputs_c, entering, precision=precise)
        ssd_out = partial_out + growth[:, :, None] * inherited
        shaped_full, norm_gate_back = jax.vjp(
            gated_norm, ssd_out, gate_half, g_gated.astype(jnp.float32)
        )
        shaped = shaped_full.astype(jnp.bfloat16)
        block_rows.append(
            (inputs + jnp.dot(shaped, w_out, preferred_element_type=jnp.float32)).astype(
                jnp.bfloat16
            )
        )
        gathered = collect(in_proj, conv_weight, conv_bias, norm_gain, gated_gain, out_proj)
        w_in, w_conv, b_conv, g_norm, g_gated, w_out = gathered
        upstream = cotangent[micro_index]
        grad_out = jnp.dot(shaped.T, upstream, preferred_element_type=jnp.float32)
        grad_shaped = jnp.dot(upstream, w_out.T, preferred_element_type=jnp.float32)
        grad_ssd, grad_gate, grad_gated = norm_gate_back(grad_shaped)
        weighted = grad_ssd * growth[:, :, None]
        local_back = jnp.einsum("thp,tn->hpn", weighted, inputs_c, precision=precise)
        grad_c = jnp.einsum("thp,hpn->tn", weighted, entering, precision=precise)
        grad_running = growth * jnp.sum(grad_ssd * inherited, axis=2)
        leaving, _ = entering_2(
            (local_back, decay_total),
            "seq",
            combine,
            (jnp.zeros_like(local_back), jnp.ones_like(decay_total)),
            True,
        )
        grad_total = decay_total * jnp.sum(leaving * entering, axis=(1, 2))
        grad_proj, grad_halo, grad_wconv, grad_bconv, grad_decay, grad_step, grad_skip = mixer_back(
            (grad_gate, grad_ssd, leaving, grad_total, grad_running, grad_c)
        )
        returned = shifted(grad_halo.astype(jnp.bfloat16), "seq", -1).astype(grad_halo.dtype)
        grad_proj = grad_proj.at[edge:, DI : DI + CD].add(returned)
        grad_low = grad_proj.astype(jnp.bfloat16)
        grad_in = jnp.dot(normed.T, grad_low, preferred_element_type=jnp.float32)
        grad_normed = jnp.dot(grad_low, w_in.T, preferred_element_type=jnp.float32)
        grad_inputs, grad_norm = norm_back(grad_normed)
        grad_rows.append((upstream.astype(jnp.float32) + grad_inputs).astype(jnp.bfloat16))
        head_totals = (
            head_totals[0] + grad_decay,
            head_totals[1] + grad_step,
            head_totals[2] + grad_skip,
        )
        current = (grad_in, grad_wconv, grad_bconv, grad_norm, grad_gated, grad_out)
        totals = (
            current if totals is None else tuple((old + new for old, new in zip(totals, current)))
        )
    shares = share_out(totals[0], totals[1], totals[2], totals[3], totals[4], totals[5])
    head_sums = lax.psum((head_totals[0], head_totals[1], head_totals[2]), ("dp", "seq"))
    return (
        jnp.stack(block_rows),
        jnp.stack(grad_rows),
        shares[0],
        shares[1],
        shares[2],
        head_sums[0],
        head_sums[1],
        head_sums[2],
        shares[3],
        shares[4],
        shares[5],
    )


def solution(mesh):
    return jax.shard_map(
        body,
        mesh=mesh,
        in_specs=(
            P("dp", "seq", None),
            P(("dp", "seq"), None),
            P(None, ("dp", "seq")),
            P(("dp", "seq")),
            P(),
            P(),
            P(),
            P(("dp", "seq")),
            P(("dp", "seq")),
            P(("dp", "seq"), None),
            P("dp", "seq", None),
        ),
        out_specs=(
            P("dp", "seq", None),
            P("dp", "seq", None),
            P(("dp", "seq"), None),
            P(None, ("dp", "seq")),
            P(("dp", "seq")),
            P(),
            P(),
            P(),
            P(("dp", "seq")),
            P(("dp", "seq")),
            P(("dp", "seq"), None),
        ),
        check_vma=False,
    )
```

profile of v0, /device:TPU:0, one launch (start us, length us, event | category | flops | bytes accessed | tf_op | source)
XLA Modules:
  0.0 1496.8 jit_solution(15407511150518520505)
XLA Ops:
  11.3 44.2 %all-reduce.40 = (bf16[1536]{0:T(1024)(128)(2,1)S(1)}, bf16[3328]{0:T(1024)(128)(2,1)S(1)}, bf16[3072]{0:T(1024)(128)(2,1)}) all-reduce(bf16[1536]{0:T(1024)(128)(2,1)S(1)} %dynamic-update-slice.5, bf16[3328]{0:T(1024)(128)(2,1)S(1)} %dynamic-update-slice.4, ...), channel_id=1, replica_groups=mesh['dp'=8,'seq'=4] {'dp','seq'}, use_global_device_ids=true, to_apply=%add.33 | all-reduce | flops 7936 | bytes 31744
  55.4 41.8 %all-gather.4 = bf16[32,104,4]{1,2,0:T(4,128)(2,1)S(1)} all-gather(bf16[1,104,4]{1,2,0:T(4,128)(2,1)} %bitcast.376), channel_id=1, replica_groups=mesh['dp'=8,'seq'=4] {'dp','seq'}, dimensions={0}, use_global_device_ids=true | all-gather | bytes 27456 | tf_op jit(solution)/shard_map/all_gather | solution.py:109
  101.7 42.9 %all-gather.14.cloned.1.call-done = bf16[1536,6448]{1,0:T(8,128)(2,1)} async-done(((bf16[48,6448]{1,0:T(8,128)(2,1)}), bf16[1536,6448]{1,0:T(8,128)(2,1)}) %all-gather.14.cloned.1.call-update) | async-done | bytes 19808272 | tf_op jit(solution)/shard_map/all_gather | solution.py:108
  144.6 14.3 fusion.195
  161.1 14.7 fusion.198
  214.4 11.9 fusion.57
  252.9 8.3 fusion.152
  314.6 19.0 %fusion.63 = f32[256,48,64]{0,2,1:T(8,128)} fusion(f32[256,48,64]{0,2,1:T(8,128)S(1)} %fusion.184, f32[256,48,64]{0,2,1:T(8,128)S(1)} %bitcast.329, f32[256,48,64]{0,2,1:T(8,128)} %fusion.159, f32[256,48]{0,1:T(8,128)S(1)} %copy-done.93, f32[256,48]{0,1:T(8,128)S(1)} %copy-done.90, f32[256,256]{1,0:T(8,128)S(1)} %copy-done.66, ...), kind=kOutput, calls=%fused_computation.110 | convolution fusion | flops 2436366336 | bytes 13058240 | tf_op jit(solution)/shard_map/jvp()/while/body/eval_jaxpr/ijh,jhp->ihp/dot_general | solution.py:50
  353.7 19.4 %fusion.65 = f32[256,48,64]{0,2,1:T(8,128)} fusion(f32[256,48,64]{0,2,1:T(8,128)S(1)} %fusion.191, f32[256,48,64]{0,2,1:T(8,128)S(1)} %bitcast.338, f32[256,48,64]{0,2,1:T(8,128)} %fusion.162, f32[256,48]{0,1:T(8,128)S(1)} %copy-done.87, f32[256,48]{0,1:T(8,128)S(1)} %copy-done.84, f32[256,256]{1,0:T(8,128)S(1)} %fusion.208, ...), kind=kOutput, calls=%fused_computation.118 | convolution fusion | flops 2436366336 | bytes 13058240 | tf_op jit(solution)/shard_map/jvp()/while/body/eval_jaxpr/ijh,jhp->ihp/dot_general | solution.py:50
  382.2 13.5 multiply_reduce_fusion.13
  395.8 15.6 %multiply_reduce_fusion.15 = (f32[3072]{0:T(1024)}, f32[256,3072]{1,0:T(8,128)}, f32[256,3072]{1,0:T(8,128)}, f32[256,3072]{1,0:T(8,128)}, f32[3072]{0:T(1024)}, /*index=5*/f32[256,3072]{1,0:T(8,128)}) fusion(f32[256,3328]{1,0:T(8,128)S(1)} %copy-done.17, f32[256,3072]{1,0:T(8,128)} %copy.364, f32[256,3072]{1,0:T(8,128)} %get-tuple-element.1374, ...), kind=kLoop, calls=%fused_computation.129 | loop fusion | flops 29878272 | bytes 44081152 | tf_op jit(solution)/shard_map/transpose(jvp())/reduce_sum | solution.py:87
  442.2 13.2 fusion.250
  455.5 26.2 %fusion.21 = (f32[256,48]{0,1:T(8,128)}, f32[256,48]{0,1:T(8,128)}, f32[256,48]{0,1:T(8,128)}, f32[256,256]{1,0:T(8,128)}, f32[256,256]{1,0:T(8,128)}, /*index=5...) fusion(f32[256,48]{0,1:T(8,128)S(1)} %copy-done.88, f32[256,48]{0,1:T(8,128)S(1)} %copy-done.85, ...), kind=kOutput, calls=%fused_computation.39 | convolution fusion | flops 2510086144 | bytes 20480000 | tf_op jit(solution)/shard_map/transpose(jvp())/while/body/eval_jaxpr/ijh,jhp->ihp/dot_general | solution.py:50
  525.7 15.4 %while.53 = (s32[]{:T(128)}, f32[48,64,128]{2,1,0:T(8,128)}, s32[]{:T(128)}, f32[4,48]{1,0:T(4,128)}, f32[4,48,64,128]{3,2,1,0:T(8,128)}, /*index=5*/s32[]{:T(128)}, s32[]{:T(128)}, s32[]{:T(128)}, s32[]{:T(128)}) while((s32[]{:T(128)}, f32[48,64,128]{2,1,0:T(8,128)}, s32[]{:T(128)}, f32[4,48]{1,0:T(4,128)}, ...), condition=%wide.region_31.33_spmd.clone, body=%wide.region_30.32_spmd.clone.sunk | while | flops 1572872 | bytes 4719343 | solution.py:38
  576.9 12.5 bitcast_add_fusion.4
  608.1 13.9 bitcast_add_fusion.5
  747.5 12.4 fusion.102
  759.9 13.6 fusion.110
  774.1 12.2 convolution_add_fusion.1
  786.5 19.2 %fusion.100 = f32[1536,6448]{1,0:T(8,128)} fusion(f32[256,6448]{1,0:T(8,128)} %scatter-add.9, f32[256]{0:T(256)S(1)} %copy-done.105, f32[1536]{0:T(1024)S(1)} %copy-done.53, bf16[2,256,1536]{2,1,0:T(8,128)(2,1)} %param.24), kind=kOutput, calls=%fused_computation.180 | convolution fusion | flops 5074137088 | bytes 47094784 | tf_op jit(solution)/shard_map/dot_general | solution.py:217
  805.6 31.2 %convolution_add_fusion = f32[1536,6448]{1,0:T(8,128)} fusion(f32[1536,6448]{1,0:T(8,128)} %fusion.100, f32[256,6448]{1,0:T(8,128)} %scatter-add.6, f32[1536]{0:T(1024)S(1)} %copy-done.53, f32[256]{0:T(256)S(1)} %copy-done.103, bf16[2,256,1536]{2,1,0:T(8,128)(2,1)} %param.24), kind=kOutput, calls=%fused_computation.12 | convolution fusion | flops 5084041216 | bytes 87202816 | tf_op jit(solution)/shard_map/dot_general | solution.py:217
  854.9 46.9 %all-reduce.43.cloned.1.call-done = (f32[4,3328]{1,0:T(4,128)}, f32[3328]{0:T(1024)}, f32[48]{0:T(128)}, f32[48]{0:T(128)}, f32[48]{0:T(128)}, /*index=5*/f32[1536]{0:T(1024)}, f32[3072]{0:T(1024)}) async-done(((f32[4,3328]{1,0:T(4,128)}, f32[3328]{0:T(1024)}, f32[48]{0:T(128)}, f32[48]{0:T(128)}, f32[48]{0:T(128)}, /*index=5*/f32[1536]{0:T(1024)}, f32[3072]{0:T(1024)}), (f32[4,3328]{1,0:T(4,128)}, ...) | async-done | bytes 85584
  907.0 209.6 %reduce-scatter.6.cloned.1.call-done = f32[96,1536]{1,0:T(8,128)} async-done(((f32[3072,1536]{1,0:T(8,128)}), f32[96,1536]{1,0:T(8,128)}) %reduce-scatter.6.cloned.1.call-update) | async-done | bytes 589840 | tf_op jit(solution)/shard_map/reduce_scatter | solution.py:124
  1116.6 369.8 %reduce-scatter.4.cloned.1.call-done = f32[48,6448]{1,0:T(8,128)} async-done(((f32[1536,6448]{1,0:T(8,128)}), f32[48,6448]{1,0:T(8,128)}) %reduce-scatter.4.cloned.1.call-update) | async-done | bytes 1238032 | tf_op jit(solution)/shard_map/reduce_scatter | solution.py:119
  (540 shorter events, 475.8 us)
Async XLA Ops:
  7.2 137.5 %all-gather.14.cloned.1.call-start = ((), (), s32[]{:S(2)}) async-start(), calls=%async_computation.2 | async-start | bytes 20680704 | tf_op jit(solution)/shard_map/all_gather | solution.py:108
  7.9 245.0 %all-gather.16.cloned.1.call-start = ((), (), s32[]{:S(2)}) async-start(), calls=%async_computation.3 | async-start | bytes 9732096 | tf_op jit(solution)/shard_map/all_gather | solution.py:113
  8.7 294.2 %all-gather.20.cloned.1.call-start = ((), (), s32[]{:S(2)}) async-start(), calls=%async_computation.7 | async-start | bytes 7864320 | tf_op jit(solution)/shard_map/all_gather | solution.py:25
  55.4 105.6 %copy-start.52 = (f32[1536]{0:T(1024)}, f32[1536]{0:T(1024)S(1)}, u32[]{:S(2)}) copy-start(f32[1536]{0:T(1024)S(1)} %convert_element_type.76) | copy-start | bytes 18436
  98.7 115.7 %copy-start.70 = (f32[3328]{0:T(1024)}, f32[3328]{0:T(1024)S(1)}, u32[]{:S(2)}) copy-start(f32[3328]{0:T(1024)S(1)} %get-tuple-element.1307) | copy-start | bytes 39940
  100.5 58.4 %copy-start.111 = (f32[256]{0:T(256)}, f32[256]{0:T(256)S(1)}, u32[]{:S(2)}) copy-start(f32[256]{0:T(256)S(1)} %get-tuple-element.1301) | copy-start | bytes 3076
  100.5 58.4 %copy-start.113 = (f32[256]{0:T(256)}, f32[256]{0:T(256)S(1)}, u32[]{:S(2)}) copy-start(f32[256]{0:T(256)S(1)} %get-tuple-element.1302) | copy-start | bytes 3076
  101.7 59.4 %copy-start.104 = (f32[256]{0:T(256)}, f32[256]{0:T(256)S(1)}, u32[]{:S(2)}) copy-start(f32[256]{0:T(256)S(1)} %fusion.224) | copy-start | bytes 3076
  101.7 57.2 %copy-start.102 = (f32[256]{0:T(256)}, f32[256]{0:T(256)S(1)}, u32[]{:S(2)}) copy-start(f32[256]{0:T(256)S(1)} %fusion.222) | copy-start | bytes 3076
  184.9 76.3 %copy-start.43 = (f32[48,2,128]{0,2,1:T(8,128)}, f32[48,2,128]{0,2,1:T(8,128)S(1)}, u32[]{:S(2)}) copy-start(f32[48,2,128]{0,2,1:T(8,128)S(1)} %copy.315) | copy-start | bytes 147460
  186.1 28.3 %collective-permute-start = (f32[3,3328]{1,0:T(4,128)}, f32[3,3328]{1,0:T(4,128)}, u32[]{:S(2)}, u32[]{:S(2)}) collective-permute-start(f32[3,3328]{1,0:T(4,128)} %copy.298), channel_id=1, source_target_pairs={{0,1},{1,2},{2,3},{4,5},{5,6},{6,7},{8,9},{9,10},{10,11},{12,13},{... | collective-permute-start | bytes 119816 | tf_op jit(solution)/shard_map/ppermute | solution.py:20
  190.0 24.4 %collective-permute-start.1 = (f32[3,3328]{1,0:T(4,128)}, f32[3,3328]{1,0:T(4,128)}, u32[]{:S(2)}, u32[]{:S(2)}) collective-permute-start(f32[3,3328]{1,0:T(4,128)} %copy.311), channel_id=1, source_target_pairs={{0,1},{1,2},{2,3},{4,5},{5,6},{6,7},{8,9},{9,10},{10,11},{12,13},{... | collective-permute-start | bytes 119816 | tf_op jit(solution)/shard_map/ppermute | solution.py:20
  237.8 104.7 %all-gather.18.cloned.1.call-start = ((), (), s32[]{:S(2)}) async-start(), calls=%async_computation.6 | async-start | bytes 7864320 | tf_op jit(solution)/shard_map/all_gather | solution.py:25
  252.0 273.7 %all-gather.24.cloned.1.call-start = ((), (), s32[]{:S(2)}) async-start(), calls=%async_computation.9 | async-start | bytes 7864320 | tf_op jit(solution)/shard_map/all_gather | solution.py:25
  292.4 162.9 %copy-start.65 = (f32[256,256]{1,0:T(8,128)}, f32[256,256]{1,0:T(8,128)S(1)}, u32[]{:S(2)}) copy-start(f32[256,256]{1,0:T(8,128)S(1)} %fusion.208) | copy-start | bytes 786436
  342.6 53.2 %copy-start.106 = (f32[256]{0:T(256)}, f32[256]{0:T(256)S(1)}, u32[]{:S(2)}) copy-start(f32[256]{0:T(256)S(1)} %fusion.225) | copy-start | bytes 3076
  382.1 135.7 %copy-start.108 = (f32[256]{0:T(256)}, f32[256]{0:T(256)S(1)}, u32[]{:S(2)}) copy-start(f32[256]{0:T(256)S(1)} %fusion.223) | copy-start | bytes 3076
  420.6 134.1 %all-gather.22.cloned.1.call-start = ((), (), s32[]{:S(2)}) async-start(), calls=%async_computation.8 | async-start | bytes 7864320 | tf_op jit(solution)/shard_map/all_gather | solution.py:25
  430.4 471.4 %all-reduce.43.cloned.1.call-start = ((), (), s32[]{:S(2)}) async-start(), calls=%async_computation.10 | async-start | bytes 183296
  681.0 51.3 %copy-start.31 = (f32[256,3328]{1,0:T(8,128)S(1)}, f32[256,3328]{1,0:T(8,128)}, u32[]{:S(2)}) copy-start(f32[256,3328]{1,0:T(8,128)} %split.20) | copy-start | bytes 10223620
  722.5 20.1 %collective-permute-start.3 = (bf16[3,3328]{1,0:T(4,128)(2,1)}, bf16[3,3328]{1,0:T(4,128)(2,1)S(1)}, u32[]{:S(2)}, u32[]{:S(2)}) collective-permute-start(bf16[3,3328]{1,0:T(4,128)(2,1)} %split.24), channel_id=1, source_target_pairs={{1,0},{2,1},{3,2},{5,4},{6,5},{7,6},{9,8},{10,9},{11,10},{13,12},{... | collective-permute-start | bytes 59912 | tf_op jit(solution)/shard_map/ppermute | solution.py:20
  723.8 20.9 %collective-permute-start.2 = (bf16[3,3328]{1,0:T(4,128)(2,1)}, bf16[3,3328]{1,0:T(4,128)(2,1)}, u32[]{:S(2)}, u32[]{:S(2)}) collective-permute-start(bf16[3,3328]{1,0:T(4,128)(2,1)} %split.25), channel_id=1, source_target_pairs={{1,0},{2,1},{3,2},{5,4},{6,5},{7,6},{9,8},{10,9},{11,10},{13,12},{... | collective-permute-start | bytes 59912 | tf_op jit(solution)/shard_map/ppermute | solution.py:20
  774.1 342.5 %reduce-scatter.6.cloned.1.call-start = ((), (), s32[]{:S(2)}) async-start(), calls=%async_computation.5 | async-start | bytes 19464192 | tf_op jit(solution)/shard_map/reduce_scatter | solution.py:124
  786.4 700.0 %reduce-scatter.4.cloned.1.call-start = ((), (), s32[]{:S(2)}) async-start(), calls=%async_computation.4 | async-start | bytes 41361408 | tf_op jit(solution)/shard_map/reduce_scatter | solution.py:119
  (121 other events, 859.2 us)
Sparse Core Ops, SparseCore 0:
  10.9 133.7 all-gather.13
  147.5 79.7 all-gather.15
  237.9 44.7 all-gather.19
  284.7 46.3 all-gather.17
  420.7 44.7 all-gather.23
  466.9 46.3 all-gather.21
  774.2 127.5 all-reduce.42
  908.8 207.7 reduce-scatter.5
  1123.6 362.7 reduce-scatter.3
where the time goes:
time: 1510 us; the launch traced here: 1500 us
  waiting for transfers between devices  671 us (44%)
  matrix products  366 us (24%)
  other arithmetic  179 us (12%)
  local copies, waits for them, and re-layouts  158 us (10%)
  blocking collectives  96.1 us (6%)
  between operations  16 us (1%)
    reduce_scatter x1, waiting for transfers between devices, share_out(): lax.psum_scatter(grad_in, ('dp', 'seq'), scatter_dimension=0, tiled=True)  370 us
    reduce_scatter x1, waiting for transfers between devices, share_out(): lax.psum_scatter(grad_out, ('dp', 'seq'), scatter_dimension=0, tiled=True)  210 us
    dot_general x6, matrix products, group_step(): output = jnp.einsum('ijh,jhp->ihp', weights, values, precision=precise)  104 us
    dot_general x2, matrix products, body(): grad_in = jnp.dot(normed.T, grad_low, preferred_element_type=jnp.float32)  50.4 us
    unnamed x10, waiting for transfers between devices  48.4 us
    unnamed x1, blocking collectives  44.2 us
    all_gather x1, waiting for transfers between devices, collect(): lax.all_gather(in_proj, ('dp', 'seq'), axis=0, tiled=True)  42.9 us
    all_gather x1, blocking collectives, collect(): lax.all_gather(conv_weight, ('dp', 'seq'), axis=1, tiled=True)  41.8 us
  transfers between devices with their start and end apart: 13, of which 4 were waited for; matrix products, arithmetic and copies ran while one was open for 28% of the time, Pallas kernels for 0%

commit v1 on v0

--- a/solution.py
+++ b/solution.py
@@ -12,6 +12,27 @@
 CD = 3328
 EPSILON = 1e-05
 precise = lax.Precision.HIGHEST
+
+
+def joined_along(blocks, dim):
+    blocks = jnp.moveaxis(blocks, 0, dim)
+    shape = blocks.shape
+    return blocks.reshape(*shape[:dim], shape[dim] * shape[dim + 1], *shape[dim + 2 :])
+
+
+def collected_by_bits(x, axis):
+    size, here = (lax.axis_size(axis), lax.axis_index(axis))
+    pieces, apart = (x[None], 1)
+    while apart < size:
+        other = lax.ppermute(pieces, axis, [(i, i ^ apart) for i in range(size)])
+        low = here & apart == 0
+        pieces = jnp.concatenate([jnp.where(low, pieces, other), jnp.where(low, other, pieces)])
+        apart *= 2
+    return pieces
+
+
+def doubled_up(shard, axis, dim):
+    return joined_along(collected_by_bits(shard, axis), dim)
 
 
 def shifted(shard, axis, by):
@@ -105,7 +126,7 @@
 
 def collect(in_proj, conv_weight, conv_bias, norm_gain, gated_gain, out_proj):
     return (
-        lax.all_gather(in_proj, ("dp", "seq"), axis=0, tiled=True),
+        doubled_up(in_proj, ("dp", "seq"), 0),
         lax.all_gather(conv_weight, ("dp", "seq"), axis=1, tiled=True),
         lax.all_gather(conv_bias, ("dp", "seq"), axis=0, tiled=True),
         lax.all_gather(norm_gain, ("dp", "seq"), axis=0, tiled=True),

time: 1510 us -> 2120 us (1.40)
  blocking collectives: 96.1 us -> 521 us
  waiting for transfers between devices: 671 us -> 816 us
  other arithmetic: 179 us -> 213 us
    unnamed x1, blocking collectives: 44.2 us -> 471 us
    ppermute x0 -> x5, waiting for transfers between devices: none -> 192 us  [collected_by_bits(): other = lax.ppermute(pieces, axis, [(i, i ^ apart) for i in range(size)])]
    all_gather x1 -> x0, waiting for transfers between devices: 42.9 us -> none  [collect(): lax.all_gather(in_proj, ('dp', 'seq'), axis=0, tiled=True)]
    unnamed x10 -> x9, waiting for transfers between devices: 48.4 us -> 45.3 us
  transfers between devices with their start and end apart: 13 -> 17, of which waited for: 4 -> 7; matrix products, arithmetic and copies ran while one was open for 28% -> 21% of each run, Pallas kernels for 0% -> 0%
where the time goes in v1:
time: 2120 us; the launch traced here: 2110 us
  waiting for transfers between devices  816 us (38%)
  blocking collectives  521 us (25%)
  matrix products  367 us (17%)
  other arithmetic  213 us (10%)
  local copies, waits for them, and re-layouts  160 us (8%)
    unnamed x1, blocking collectives  471 us
    reduce_scatter x1, waiting for transfers between devices, share_out(): lax.psum_scatter(grad_in, ('dp', 'seq'), scatter_dimension=0, tiled=True)  370 us
    reduce_scatter x1, waiting for transfers between devices, share_out(): lax.psum_scatter(grad_out, ('dp', 'seq'), scatter_dimension=0, tiled=True)  210 us
    ppermute x5, waiting for transfers between devices, collected_by_bits(): other = lax.ppermute(pieces, axis, [(i, i ^ apart) for i in range(size)])  192 us
    dot_general x6, matrix products, group_step(): output = jnp.einsum('ijh,jhp->ihp', weights, values, precision=precise)  104 us
    dot_general x2, matrix products, body(): grad_in = jnp.dot(normed.T, grad_low, preferred_element_type=jnp.float32)  50.2 us
    unnamed x9, waiting for transfers between devices  45.3 us
  transfers between devices with their start and end apart: 17, of which 7 were waited for; matrix products, arithmetic and copies ran while one was open for 21% of the time, Pallas kernels for 0%

profile of v1, /device:TPU:0, one launch (start us, length us, event | category | flops | bytes accessed | tf_op | source)
XLA Modules:
  0.0 2111.2 jit_solution(12488806520332102096)
XLA Ops:
  14.9 28.1 %collective-permute-done.1 = bf16[2,48,6448]{2,1,0:T(8,128)(2,1)S(1)} collective-permute-done((bf16[2,48,6448]{2,1,0:T(8,128)(2,1)}, bf16[2,48,6448]{2,1,0:T(8,128)(2,1)S(1)}, u32[]{:S(2)}, u32[]{:S(2)}) %collective-permute-start.1) | collective-permute-done | bytes 1238048 | tf_op jit(solution)/shard_map/ppermute | solution.py:27
  46.5 54.2 %collective-permute-done.2 = bf16[4,48,6448]{2,1,0:T(8,128)(2,1)} collective-permute-done((bf16[4,48,6448]{2,1,0:T(8,128)(2,1)S(1)}, bf16[4,48,6448]{2,1,0:T(8,128)(2,1)}, u32[]{:S(2)}, u32[]{:S(2)}) %collective-permute-start.2) | collective-permute-done | bytes 2476064 | tf_op jit(solution)/shard_map/ppermute | solution.py:27
  108.2 107.5 %collective-permute-done.3 = bf16[8,48,6448]{2,1,0:T(8,128)(2,1)} collective-permute-done((bf16[8,48,6448]{2,1,0:T(8,128)(2,1)}, bf16[8,48,6448]{2,1,0:T(8,128)(2,1)}, u32[]{:S(2)}, u32[]{:S(2)}) %collective-permute-start.3) | collective-permute-done | bytes 4952096 | tf_op jit(solution)/shard_map/ppermute | solution.py:27
  229.9 470.5 %all-reduce.40 = (bf16[1536]{0:T(1024)(128)(2,1)S(1)}, bf16[3328]{0:T(1024)(128)(2,1)S(1)}, bf16[3072]{0:T(1024)(128)(2,1)}) all-reduce(bf16[1536]{0:T(1024)(128)(2,1)S(1)} %dynamic-update-slice.5, bf16[3328]{0:T(1024)(128)(2,1)S(1)} %dynamic-update-slice.4, ...), channel_id=1, replica_groups=mesh['dp'=8,'seq'=4] {'dp','seq'}, use_global_device_ids=true, to_apply=%add.33 | all-reduce | flops 7936 | bytes 31744
  700.4 40.0 %all-gather.4 = bf16[32,104,4]{1,2,0:T(4,128)(2,1)S(1)} all-gather(bf16[1,104,4]{1,2,0:T(4,128)(2,1)S(1)} %bitcast.437), channel_id=1, replica_groups=mesh['dp'=8,'seq'=4] {'dp','seq'}, dimensions={0}, use_global_device_ids=true | all-gather | bytes 27456 | tf_op jit(solution)/shard_map/all_gather | solution.py:130
  761.2 14.8 fusion.167
  778.0 14.7 fusion.164
  930.6 19.0 fusion.63
  969.7 19.2 fusion.65
  998.0 13.5 multiply_reduce_fusion.13
  1011.6 15.6 multiply_reduce_fusion.15
  1058.3 13.2 fusion.276
  1071.6 26.1 %fusion.21 = (f32[256,48]{0,1:T(8,128)}, f32[256,48]{0,1:T(8,128)}, f32[256,48]{0,1:T(8,128)}, f32[256,256]{1,0:T(8,128)}, f32[256,256]{1,0:T(8,128)}, /*index=5...) fusion(f32[256,48]{0,1:T(8,128)S(1)} %copy-done.93, f32[256,48]{0,1:T(8,128)S(1)} %copy-done.90, ...), kind=kOutput, calls=%fused_computation.43 | convolution fusion | flops 2510086144 | bytes 20480000 | tf_op jit(solution)/shard_map/transpose(jvp())/while/body/eval_jaxpr/ijh,jhp->ihp/dot_general | solution.py:71
  1141.6 15.4 while.53
  1193.1 12.5 bitcast_add_fusion.4
  1224.2 13.9 bitcast_add_fusion.5
  1361.0 12.4 fusion.110
  1376.2 13.6 fusion.118
  1390.4 12.3 convolution_add_fusion.1
  1402.8 19.1 fusion.108
  1421.9 31.2 %convolution_add_fusion = f32[1536,6448]{1,0:T(8,128)} fusion(f32[1536,6448]{1,0:T(8,128)} %fusion.108, f32[256,6448]{1,0:T(8,128)} %scatter-add.6, f32[256]{0:T(256)S(1)} %copy-done.108, f32[1536]{0:T(1024)S(1)} %copy-done.58, bf16[2,256,1536]{2,1,0:T(8,128)(2,1)} %param.24), kind=kOutput, calls=%fused_computation.12 | convolution fusion | flops 5084041216 | bytes 87202816 | tf_op jit(solution)/shard_map/dot_general | solution.py:238
  1471.0 45.1 %all-reduce.43.cloned.1.call-done = (f32[4,3328]{1,0:T(4,128)}, f32[3328]{0:T(1024)}, f32[48]{0:T(128)}, f32[48]{0:T(128)}, f32[48]{0:T(128)}, /*index=5*/f32[1536]{0:T(1024)}, f32[3072]{0:T(1024)}) async-done(((f32[4,3328]{1,0:T(4,128)}, f32[3328]{0:T(1024)}, f32[48]{0:T(128)}, f32[48]{0:T(128)}, f32[48]{0:T(128)}, /*index=5*/f32[1536]{0:T(1024)}, f32[3072]{0:T(1024)}), (f32[4,3328]{1,0:T(4,128)}, ...) | async-done | bytes 85584
  1521.3 209.6 %reduce-scatter.6.cloned.1.call-done = f32[96,1536]{1,0:T(8,128)} async-done(((f32[3072,1536]{1,0:T(8,128)}), f32[96,1536]{1,0:T(8,128)}) %reduce-scatter.6.cloned.1.call-update) | async-done | bytes 589840 | tf_op jit(solution)/shard_map/reduce_scatter | solution.py:145
  1730.9 369.7 %reduce-scatter.4.cloned.1.call-done = f32[48,6448]{1,0:T(8,128)} async-done(((f32[1536,6448]{1,0:T(8,128)}), f32[48,6448]{1,0:T(8,128)}) %reduce-scatter.4.cloned.1.call-update) | async-done | bytes 1238032 | tf_op jit(solution)/shard_map/reduce_scatter | solution.py:140
  (577 shorter events, 540.4 us)
Async XLA Ops:
  7.2 861.6 %all-gather.13.cloned.1.call-start = ((), (), s32[]{:S(2)}) async-start(), calls=%async_computation.2 | async-start | bytes 9732096 | tf_op jit(solution)/shard_map/all_gather | solution.py:134
  7.2 2.5 collective-permute-start
  12.1 30.9 %collective-permute-start.1 = (bf16[2,48,6448]{2,1,0:T(8,128)(2,1)}, bf16[2,48,6448]{2,1,0:T(8,128)(2,1)S(1)}, u32[]{:S(2)}, u32[]{:S(2)}) collective-permute-start(bf16[2,48,6448]{2,1,0:T(8,128)(2,1)} %pad_maximum_fusion.8), channel_id=1, source_target_pairs={{0,2},{1,3},{2,0},{3,1},{4,6},{5,7},{6,4},{7,5},{8,10},{9,11},{10,... | collective-permute-start | bytes 3714056 | tf_op jit(solution)/shard_map/ppermute | solution.py:27
  44.7 56.0 %collective-permute-start.2 = (bf16[4,48,6448]{2,1,0:T(8,128)(2,1)S(1)}, bf16[4,48,6448]{2,1,0:T(8,128)(2,1)}, u32[]{:S(2)}, u32[]{:S(2)}) collective-permute-start(bf16[4,48,6448]{2,1,0:T(8,128)(2,1)S(1)} %pad_maximum_fusion.5), channel_id=1, source_target_pairs={{0,4},{1,5},{2,6},{3,7},{4,0},{5,1},{6,2},{7,3},{8,12},{9,13},{10,... | collective-permute-start | bytes 7428104 | tf_op jit(solution)/shard_map/ppermute | solution.py:27
  106.7 109.1 %collective-permute-start.3 = (bf16[8,48,6448]{2,1,0:T(8,128)(2,1)}, bf16[8,48,6448]{2,1,0:T(8,128)(2,1)}, u32[]{:S(2)}, u32[]{:S(2)}) collective-permute-start(bf16[8,48,6448]{2,1,0:T(8,128)(2,1)} %pad_maximum_fusion.2), channel_id=1, source_target_pairs={{0,8},{1,9},{2,10},{3,11},{4,12},{5,13},{6,14},{7,15},{8,0},{9,1},... | collective-permute-start | bytes 14856200 | tf_op jit(solution)/shard_map/ppermute | solution.py:27
  219.9 480.5 %copy-start.128 = (bf16[4,104]{1,0:T(4,128)(2,1)S(1)}, bf16[4,104]{1,0:T(4,128)(2,1)}, u32[]{:S(2)}) copy-start(bf16[4,104]{1,0:T(4,128)(2,1)} %param.26) | copy-start | bytes 2500
  220.0 521.9 %copy-start.30 = (bf16[2,256,1536]{2,1,0:T(8,128)(2,1)S(1)}, bf16[2,256,1536]{2,1,0:T(8,128)(2,1)}, u32[]{:S(2)}) copy-start(bf16[2,256,1536]{2,1,0:T(8,128)(2,1)} %param.24) | copy-start | bytes 4718596
  220.0 522.3 %copy-start.135 = (f32[48]{0:T(128)S(1)}, f32[48]{0:T(128)}, u32[]{:S(2)}) copy-start(f32[48]{0:T(128)} %param.28) | copy-start | bytes 580
  226.8 516.1 %collective-permute-start.4 = (bf16[16,48,6448]{2,1,0:T(8,128)(2,1)}, bf16[16,48,6448]{2,1,0:T(8,128)(2,1)}, u32[]{:S(2)}, u32[]{:S(2)}) collective-permute-start(bf16[16,48,6448]{2,1,0:T(8,128)(2,1)} %pad_maximum_fusion.1), channel_id=1, source_target_pairs={{0,16},{1,17},{2,18},{3,19},{4,20},{5,21},{6,22},{7,23},{8,24},{9,... | collective-permute-start | bytes 29712392 | tf_op jit(solution)/shard_map/ppermute | solution.py:27
  229.1 689.9 %all-gather.17.cloned.1.call-start = ((), (), s32[]{:S(2)}) async-start(), calls=%async_computation.6 | async-start | bytes 7864320 | tf_op jit(solution)/shard_map/all_gather | solution.py:46
  700.4 77.6 %copy-start.57 = (f32[1536]{0:T(1024)}, f32[1536]{0:T(1024)S(1)}, u32[]{:S(2)}) copy-start(f32[1536]{0:T(1024)S(1)} %convert_element_type.93) | copy-start | bytes 18436
  741.8 88.0 %copy-start.75 = (f32[3328]{0:T(1024)}, f32[3328]{0:T(1024)S(1)}, u32[]{:S(2)}) copy-start(f32[3328]{0:T(1024)S(1)} %get-tuple-element.1307) | copy-start | bytes 39940
  803.0 26.8 %collective-permute-start.5 = (f32[3,3328]{1,0:T(4,128)}, f32[3,3328]{1,0:T(4,128)}, u32[]{:S(2)}, u32[]{:S(2)}) collective-permute-start(f32[3,3328]{1,0:T(4,128)} %copy.298), channel_id=1, source_target_pairs={{0,1},{1,2},{2,3},{4,5},{5,6},{6,7},{8,9},{9,10},{10,11},{12,13},{... | collective-permute-start | bytes 119816 | tf_op jit(solution)/shard_map/ppermute | solution.py:41
  807.0 22.8 %collective-permute-start.6 = (f32[3,3328]{1,0:T(4,128)}, f32[3,3328]{1,0:T(4,128)}, u32[]{:S(2)}, u32[]{:S(2)}) collective-permute-start(f32[3,3328]{1,0:T(4,128)} %copy.311), channel_id=1, source_target_pairs={{0,1},{1,2},{2,3},{4,5},{5,6},{6,7},{8,9},{9,10},{10,11},{12,13},{... | collective-permute-start | bytes 119816 | tf_op jit(solution)/shard_map/ppermute | solution.py:41
  853.3 105.3 %all-gather.15.cloned.1.call-start = ((), (), s32[]{:S(2)}) async-start(), calls=%async_computation.5 | async-start | bytes 7864320 | tf_op jit(solution)/shard_map/all_gather | solution.py:46
  867.6 274.0 %all-gather.21.cloned.1.call-start = ((), (), s32[]{:S(2)}) async-start(), calls=%async_computation.8 | async-start | bytes 7864320 | tf_op jit(solution)/shard_map/all_gather | solution.py:46
  908.5 162.9 %copy-start.70 = (f32[256,256]{1,0:T(8,128)}, f32[256,256]{1,0:T(8,128)S(1)}, u32[]{:S(2)}) copy-start(f32[256,256]{1,0:T(8,128)S(1)} %fusion.234) | copy-start | bytes 786436
  998.0 135.7 %copy-start.113 = (f32[256]{0:T(256)}, f32[256]{0:T(256)S(1)}, u32[]{:S(2)}) copy-start(f32[256]{0:T(256)S(1)} %fusion.249) | copy-start | bytes 3076
  1036.4 134.1 %all-gather.19.cloned.1.call-start = ((), (), s32[]{:S(2)}) async-start(), calls=%async_computation.7 | async-start | bytes 7864320 | tf_op jit(solution)/shard_map/all_gather | solution.py:46
  1046.5 469.7 %all-reduce.43.cloned.1.call-start = ((), (), s32[]{:S(2)}) async-start(), calls=%async_computation.9 | async-start | bytes 183296
  1338.5 20.1 collective-permute-start.8
  1339.8 33.5 %collective-permute-start.7 = (bf16[3,3328]{1,0:T(4,128)(2,1)}, bf16[3,3328]{1,0:T(4,128)(2,1)}, u32[]{:S(2)}, u32[]{:S(2)}) collective-permute-start(bf16[3,3328]{1,0:T(4,128)(2,1)} %split.25), channel_id=1, source_target_pairs={{1,0},{2,1},{3,2},{5,4},{6,5},{7,6},{9,8},{10,9},{11,10},{13,12},{... | collective-permute-start | bytes 59912 | tf_op jit(solution)/shard_map/ppermute | solution.py:41
  1390.4 340.6 %reduce-scatter.6.cloned.1.call-start = ((), (), s32[]{:S(2)}) async-start(), calls=%async_computation.4 | async-start | bytes 19464192 | tf_op jit(solution)/shard_map/reduce_scatter | solution.py:145
  1402.8 697.9 %reduce-scatter.4.cloned.1.call-start = ((), (), s32[]{:S(2)}) async-start(), calls=%async_computation.3 | async-start | bytes 41361408 | tf_op jit(solution)/shard_map/reduce_scatter | solution.py:140
  (135 other events, 1155.3 us)
Sparse Core Ops, SparseCore 0:
  229.2 487.9 all-gather.12
  853.4 42.2 all-gather.16
  897.8 46.3 all-gather.14
  1036.5 42.4 all-gather.20
  1080.5 46.3 all-gather.18
  1390.5 125.6 all-reduce.42
  1523.2 207.7 reduce-scatter.5
  1737.9 362.6 reduce-scatter.3
